TPU v7x, 32 devices: a whole 2x2x4 slice. The times are simulated.
32 devices in a mesh: row: 4 (over z), col: 8 (over y, x, core).
Axes of the slice: x: 2, y: 2, z: 4, core: 2. Of those that a mesh axis runs over, the one named last changes fastest.
Arguments:
- tokens: bfloat16 [2048, 2048], P(('row', 'col')), may hold values from -6 to 6
- timestep: int32 [1], replicated, may hold values from 0 to 999
- mod_weight: float32 [256, 2048], replicated, may hold values from -0.375 to 0.375
- qkv_weight: bfloat16 [3, 2048, 2048], P(None, None, 'col'), may hold values from -0.125 to 0.125
- attn_scale: float32 [16], P('col'), may hold values from 4 to 40
- out_weight: bfloat16 [2048, 2048], P('col'), may hold values from -0.5 to 0.5
- grad_update: bfloat16 [2048, 2048], P(('row', 'col')), may hold values from -6 to 6
Outputs:
- update: bfloat16 [2048, 2048], P(('row', 'col'))
- grad_tokens: bfloat16 [2048, 2048], P(('row', 'col'))
- grad_qkv: float32 [3, 2048, 2048], P(None, 'row', 'col')
- grad_out: float32 [2048, 2048], P('col', 'row')
All inputs are finite; a program needn't handle non-finite values.
Results may differ from a plain program's by a relative error of at most 0.018.
Values may be sent and summed in bfloat16 or wider, within the bound.
A program may use at most 128 MiB of HBM per device.

v0:
```python
import math
import jax
import jax.numpy as jnp
from jax import lax
from jax.sharding import PartitionSpec as P

epsilon = 1e-06


def embed(timestep, count):
    index = jnp.arange(count, dtype=jnp.float32)
    freqs = jnp.exp(-math.log(10000.0) * index / count)
    angles = timestep.astype(jnp.float32)[0] * freqs
    return jnp.concatenate([jnp.cos(angles), jnp.sin(angles)])


def unit_rows(values):
    factor = lax.rsqrt(jnp.mean(values * values, -1, keepdims=True) + epsilon)
    return (values * factor, factor)


def unit_grad(grad_unit, unit, factor):
    return factor * (grad_unit - unit * jnp.mean(grad_unit * unit, -1, keepdims=True))


def split_blocks(array, size):
    return array.reshape((array.shape[0] // size, size) + array.shape[1:])


def per_device(tokens, timestep, mod_weight, qkv_weight, attn_scale, out_weight, grad_update):
    tok_dev, width = tokens.shape
    heads_here = attn_scale.shape[0]
    inner = qkv_weight.shape[2]
    head_dim = inner // heads_here
    span = tok_dev * lax.axis_size("col")
    coeff = attn_scale / head_dim
    embedded = embed(timestep, mod_weight.shape[0] // 2)
    gain = 1.0 + jnp.sum(embedded[:, None] * mod_weight, 0)
    tok_float = tokens.astype(jnp.float32)
    rstd = lax.rsqrt(jnp.mean(tok_float * tok_float, -1, keepdims=True) + epsilon)
    normed = tok_float * rstd
    hidden = (normed * gain).astype(jnp.bfloat16)
    group = lax.all_gather(hidden, "col", axis=0, tiled=True)
    raw = jnp.einsum("sd,kdh->ksh", group, qkv_weight, preferred_element_type=jnp.float32)
    query_unit, query_factor = unit_rows(raw[0].reshape(span, heads_here, head_dim))
    key_unit, key_factor = unit_rows(raw[1].reshape(span, heads_here, head_dim))
    queries = query_unit.astype(jnp.bfloat16)
    key_heads = key_unit.astype(jnp.bfloat16)
    value_heads = raw[2].astype(jnp.bfloat16).reshape(span, heads_here, head_dim)
    start_state = (
        jnp.zeros((heads_here, span), jnp.float32),
        jnp.zeros((span, heads_here, head_dim), jnp.float32),
    )
    carry = start_state
    key_piece = lax.all_gather(key_heads, "row", axis=0, tiled=True)
    value_piece = lax.all_gather(value_heads, "row", axis=0, tiled=True)
    size = math.gcd(key_piece.shape[0], 512)

    def attend_step(state, block):
        key_block, value_block = block
        scores = (
            jnp.einsum("qhd,khd->hqk", queries, key_block, preferred_element_type=jnp.float32)
            * coeff[:, None, None]
        )
        weights = jnp.exp(scores - attn_scale[:, None, None])
        totals = state[0] + jnp.sum(weights, -1)
        mixed = state[1] + jnp.einsum(
            "hqk,khd->qhd",
            weights.astype(jnp.bfloat16),
            value_block,
            preferred_element_type=jnp.float32,
        )
        return ((totals, mixed), None)

    carry, unused = lax.scan(
        attend_step, carry, (split_blocks(key_piece, size), split_blocks(value_piece, size))
    )
    totals, mixed = carry
    attended_heads = (mixed / totals.T[:, :, None]).astype(jnp.bfloat16)
    attended = attended_heads.reshape(span, inner)
    rows = attended
    update = lax.psum_scatter(
        jnp.dot(rows, out_weight, preferred_element_type=jnp.float32).astype(jnp.bfloat16),
        "col",
        scatter_dimension=0,
        tiled=True,
    )
    grad_group = lax.all_gather(grad_update, "col", axis=0, tiled=True)
    out_part = lax.dot_general(
        attended, grad_group, (((0,), (0,)), ((), ())), preferred_element_type=jnp.float32
    )
    grad_out = lax.psum_scatter(
        out_part.astype(jnp.bfloat16), "row", scatter_dimension=1, tiled=True
    ).astype(jnp.float32)
    grad_attended = lax.dot_general(
        grad_group, out_weight, (((1,), (1,)), ((), ())), preferred_element_type=jnp.float32
    ).astype(jnp.bfloat16)
    grad_heads = grad_attended.reshape(span, heads_here, head_dim)
    delta = jnp.sum(grad_heads.astype(jnp.float32) * attended_heads.astype(jnp.float32), -1)
    inverse = 1.0 / totals

    def pair_terms(query_rows, grad_rows, inverse_rows, delta_rows, key_block, value_block):
        scores = (
            jnp.einsum("qhd,khd->hqk", query_rows, key_block, preferred_element_type=jnp.float32)
            * coeff[:, None, None]
        )
        probs = jnp.exp(scores - attn_scale[:, None, None]) * inverse_rows[:, :, None]
        dprobs = jnp.einsum(
            "qhd,khd->hqk", grad_rows, value_block, preferred_element_type=jnp.float32
        )
        dscores = (probs * (dprobs - delta_rows[:, :, None]) * coeff[:, None, None]).astype(
            jnp.bfloat16
        )
        return (probs, dscores)

    empty_own = jnp.zeros((span, heads_here, head_dim), jnp.float32)
    carry = empty_own
    key_piece = lax.all_gather(key_heads, "row", axis=0, tiled=True)
    value_piece = lax.all_gather(value_heads, "row", axis=0, tiled=True)
    size = math.gcd(key_piece.shape[0], 512)

    def query_step(state, block):
        key_block, value_block = block
        probs, dscores = pair_terms(queries, grad_heads, inverse, delta.T, key_block, value_block)
        return (
            state
            + jnp.einsum("hqk,khd->qhd", dscores, key_block, preferred_element_type=jnp.float32),
            None,
        )

    carry, unused = lax.scan(
        query_step, carry, (split_blocks(key_piece, size), split_blocks(value_piece, size))
    )
    grad_query = carry
    all_inverse, all_delta = (
        lax.all_gather(inverse.T, "row", axis=0, tiled=True),
        lax.all_gather(delta, "row", axis=0, tiled=True),
    )
    carry = (empty_own, empty_own)
    query_piece = lax.all_gather(queries, "row", axis=0, tiled=True)
    grad_piece = lax.all_gather(grad_heads, "row", axis=0, tiled=True)
    count = query_piece.shape[0]
    size = math.gcd(count, 512)

    def key_step(state, block):
        query_block, grad_block, inverse_block, delta_block = block
        probs, dscores = pair_terms(
            query_block, grad_block, inverse_block.T, delta_block.T, key_heads, value_heads
        )
        grad_key = state[0] + jnp.einsum(
            "hqk,qhd->khd", dscores, query_block, preferred_element_type=jnp.float32
        )
        grad_value = state[1] + jnp.einsum(
            "hqk,qhd->khd",
            probs.astype(jnp.bfloat16),
            grad_block,
            preferred_element_type=jnp.float32,
        )
        return ((grad_key, grad_value), None)

    carry, unused = lax.scan(
        key_step,
        carry,
        (
            split_blocks(query_piece, size),
            split_blocks(grad_piece, size),
            split_blocks(all_inverse, size),
            split_blocks(all_delta, size),
        ),
    )
    grad_key, grad_value = carry
    grad_q = (
        unit_grad(grad_query, query_unit, query_factor).astype(jnp.bfloat16).reshape(span, inner)
    )
    grad_k = unit_grad(grad_key, key_unit, key_factor).astype(jnp.bfloat16).reshape(span, inner)
    grad_v = grad_value.astype(jnp.bfloat16).reshape(span, inner)
    grad_raw = jnp.stack([grad_q, grad_k, grad_v])
    qkv_part = jnp.einsum("sd,ksh->kdh", group, grad_raw, preferred_element_type=jnp.float32)
    grad_qkv = lax.psum_scatter(
        qkv_part.astype(jnp.bfloat16), "row", scatter_dimension=1, tiled=True
    ).astype(jnp.float32)
    rows = grad_raw
    grad_hidden = lax.psum_scatter(
        jnp.einsum("ksh,kdh->sd", rows, qkv_weight, preferred_element_type=jnp.float32).astype(
            jnp.bfloat16
        ),
        "col",
        scatter_dimension=0,
        tiled=True,
    ).astype(jnp.float32)
    grad_normed = grad_hidden * gain
    grad_tokens = (
        rstd * (grad_normed - normed * jnp.mean(grad_normed * normed, -1, keepdims=True))
    ).astype(jnp.bfloat16)
    return (update, grad_tokens, grad_qkv, grad_out)


def solution(mesh):
    placed = (
        P(("row", "col"), None),
        P(),
        P(),
        P(None, None, "col"),
        P("col"),
        P("col", None),
        P(("row", "col"), None),
    )
    return jax.shard_map(
        per_device,
        mesh=mesh,
        in_specs=placed,
        out_specs=(
            P(("row", "col"), None),
            P(("row", "col"), None),
            P(None, "row", "col"),
            P("col", "row"),
        ),
        check_vma=False,
    )
```

profile of v0, /device:TPU:0, one launch (start us, length us, event | category | flops | bytes accessed | tf_op | source)
XLA Modules:
  0.0 422.1 jit_solution(2159010349905390229)
XLA Ops:
  11.1 30.6 %all-gather.7.cloned.1.call-done = bf16[512,2048]{1,0:T(8,128)(2,1)} async-done(((bf16[64,2048]{1,0:T(8,128)(2,1)}), bf16[512,2048]{1,0:T(8,128)(2,1)}) %all-gather.7.cloned.1.call-update) | async-done | bytes 2097168 | tf_op jit(solution)/shard_map/all_gather | solution.py:43
  41.7 3.4 fusion.54
  60.4 16.5 %all-gather.9.cloned.1.call-done = bf16[2048,2,128]{0,2,1:T(8,128)(2,1)} async-done(((bf16[512,2,128]{0,2,1:T(8,128)(2,1)}), bf16[2048,2,128]{0,2,1:T(8,128)(2,1)}) %all-gather.9.cloned.1.call-update) | async-done | bytes 1048592 | tf_op jit(solution)/shard_map/all_gather | solution.py:55
  82.3 23.6 %all-gather.11.cloned.1.call-done = bf16[2048,2,128]{0,2,1:T(8,128)(2,1)} async-done(((bf16[512,2,128]{0,2,1:T(8,128)(2,1)}), bf16[2048,2,128]{0,2,1:T(8,128)(2,1)}) %all-gather.11.cloned.1.call-update) | async-done | bytes 1048592 | tf_op jit(solution)/shard_map/all_gather | solution.py:56
  105.9 3.7 copy.32
  109.5 32.0 %while.37 = (s32[]{:T(128)}, f32[2,512]{1,0:T(2,128)S(1)}, f32[512,2,128]{0,2,1:T(8,128)}, bf16[4,512,2,128]{3,1,2,0:T(8,128)(2,1)}, bf16[512,2,128]{2,0,1:T(8,1...) while((s32[]{:T(128)}, f32[2,512]{1,0:T(2,128)S(1)}, ...), condition=%wide.region_6.7_spmd.clone, body=%wide.region_4.6_spmd.clone.sunk | while | flops 271844352 | bytes 8143544 | solution.py:75
  141.5 3.5 multiply_reduce_fusion.3
  151.2 33.2 %while.38 = (s32[]{:T(128)}, f32[512,2,128]{0,2,1:T(8,128)}, bf16[4,512,2,128]{1,3,2,0:T(8,128)(2,1)}, bf16[512,2,128]{2,1,0:T(2,128)(2,1)S(1)}, f32[2]{0:T(128)...) while((s32[]{:T(128)}, f32[512,2,128]{0,2,1:T(8,128)}, ...), condition=%wide.region_10.11_spmd.clone, body=%wide.region_9.10_spmd.clone.sunk | while | flops 406585344 | bytes 7087251 | solution.py:131
  155.9 3.6 fusion.110
  164.1 3.6 fusion.110
  172.4 3.8 fusion.110
  180.8 3.6 fusion.110
  190.8 13.2 %all_gather.33 = f32[2048,2]{0,1:T(2,128)S(1)} all-gather(f32[512,2]{0,1:T(2,128)S(1)} %get-tuple-element.734), channel_id=1, replica_groups=mesh['row'=4,'col'=8] {'row'}, dimensions={0}, use_global_device_ids=true | all-gather | bytes 20480 | tf_op jit(solution)/shard_map/all_gather | solution.py:137
  204.0 13.2 %all_gather.31 = f32[2048,2]{0,1:T(2,128)S(1)} all-gather(f32[512,2]{0,1:T(2,128)S(1)} %fusion.81), channel_id=1, replica_groups=mesh['row'=4,'col'=8] {'row'}, dimensions={0}, use_global_device_ids=true | all-gather | bytes 20480 | tf_op jit(solution)/shard_map/all_gather | solution.py:136
  217.2 3.4 convolution_convert_fusion.2
  220.9 36.4 %while.39 = (s32[]{:T(128)}, f32[512,2,128]{0,2,1:T(8,128)}, f32[512,2,128]{0,2,1:T(8,128)}, bf16[4,512,2,128]{3,1,0,2:T(8,128)(2,1)}, bf16[512,2,128]{2,0,1:T(8...) while((s32[]{:T(128)}, f32[512,2,128]{0,2,1:T(8,128)}, ...), condition=%wide.region_13.14_spmd.clone, body=%wide.region_12.13_spmd.clone.sunk | while | flops 541589504 | bytes 9988260 | solution.py:161
  235.8 3.3 fusion.118
  244.9 3.3 fusion.118
  262.7 4.3 %bitcast_convert_fusion.2 = bf16[512,2048]{1,0:T(8,128)(2,1)} fusion(bf16[3,2048,256]{2,1,0:T(8,128)(2,1)S(1)} %copy-done, bf16[1,512,256]{2,1,0:T(8,128)(2,1)} %copy.59, bf16[1,512,256]{2,1,0:T(8,128)(2,1)} %copy.58, bf16[1,512,256]{2,1,0:T(8,128)(2,1)} %stack_reshape.9), kind=kOutput, calls=%fused_computation.57 | convolution fusion | flops 1612447744 | bytes 6029312 | tf_op jit(solution)/shard_map/ksh,kdh->sd/dot_general | solution.py:184
  268.0 5.2 %fusion.50 = bf16[3,2048,256]{1,2,0:T(8,128)(2,1)} fusion(bf16[512,2048]{1,0:T(8,128)(2,1)} %all-gather.7.cloned.1.call-done, bf16[1,512,256]{2,1,0:T(8,128)(2,1)} %copy.59, bf16[1,512,256]{2,1,0:T(8,128)(2,1)} %copy.58, bf16[1,512,256]{2,1,0:T(8,128)(2,1)S(1)} %copy-done.11), kind=kOutput, calls=%fused_computation.60 | convolution fusion | flops 1612972032 | bytes 6029312 | tf_op jit(solution)/shard_map/sd,ksh->kdh/dot_general | solution.py:178
  274.2 3.4 convolution_convert_fusion.1
  279.5 28.2 %reduce-scatter.7.cloned.1.call-done = bf16[64,2048]{1,0:T(8,128)(2,1)} async-done(((bf16[512,2048]{1,0:T(8,128)(2,1)}), bf16[64,2048]{1,0:T(8,128)(2,1)}) %reduce-scatter.7.cloned.1.call-update) | async-done | bytes 262160 | tf_op jit(solution)/shard_map/reduce_scatter | solution.py:183
  310.8 59.7 %reduce-scatter.9.cloned.1.call-done = bf16[3,512,256]{1,2,0:T(8,128)(2,1)} async-done(((bf16[3,2048,256]{1,2,0:T(8,128)(2,1)}), bf16[3,512,256]{1,2,0:T(8,128)(2,1)}) %reduce-scatter.9.cloned.1.call-update) | async-done | bytes 786448 | tf_op jit(solution)/shard_map/reduce_scatter | solution.py:179
  373.0 42.2 %reduce-scatter.5.cloned.1.call-done = bf16[64,2048]{1,0:T(8,128)(2,1)} async-done(((bf16[512,2048]{1,0:T(8,128)(2,1)}), bf16[64,2048]{1,0:T(8,128)(2,1)}) %reduce-scatter.5.cloned.1.call-update) | async-done | bytes 262160 | tf_op jit(solution)/shard_map/reduce_scatter | solution.py:82
  (147 shorter events, 131.1 us)
Async XLA Ops:
  7.2 34.6 %copy-start = (bf16[3,2048,256]{2,1,0:T(8,128)(2,1)S(1)}, bf16[3,2048,256]{2,1,0:T(8,128)(2,1)}, u32[]{:S(2)}) copy-start(bf16[3,2048,256]{2,1,0:T(8,128)(2,1)} %param.16) | copy-start | bytes 9437188
  7.2 2.9 copy-start.7
  7.2 34.5 %all-gather.7.cloned.1.call-start = ((), (), s32[]{:S(2)}) async-start(), calls=%async_computation.4 | async-start | bytes 2359296 | tf_op jit(solution)/shard_map/all_gather | solution.py:43
  11.1 65.8 %all-gather.9.cloned.1.call-start = ((), (), s32[]{:S(2)}) async-start(), calls=%async_computation.5 | async-start | bytes 1310720 | tf_op jit(solution)/shard_map/all_gather | solution.py:55
  45.2 1.1 copy-start.10
  46.3 5.0 %copy-start.12 = (f32[2]{0:T(128)S(1)}, f32[2]{0:T(128)}, u32[]{:S(2)}) copy-start(f32[2]{0:T(128)} %param.17) | copy-start | bytes 28
  48.8 57.1 %all-gather.11.cloned.1.call-start = ((), (), s32[]{:S(2)}) async-start(), calls=%async_computation.6 | async-start | bytes 1310720 | tf_op jit(solution)/shard_map/all_gather | solution.py:56
  50.6 90.9 %all-gather.13.cloned.1.call-start = ((), (), s32[]{:S(2)}) async-start(), calls=%async_computation.8 | async-start | bytes 2359296 | tf_op jit(solution)/shard_map/all_gather | solution.py:88
  51.2 169.7 %all-gather.15.cloned.1.call-start = ((), (), s32[]{:S(2)}) async-start(), calls=%async_computation.9 | async-start | bytes 1310720 | tf_op jit(solution)/shard_map/all_gather | solution.py:140
  59.4 1.0 copy-start.1
  60.4 160.5 %all-gather.17.cloned.1.call-start = ((), (), s32[]{:S(2)}) async-start(), calls=%async_computation.10 | async-start | bytes 1310720 | tf_op jit(solution)/shard_map/all_gather | solution.py:141
  79.5 30.0 %copy-start.2 = (bf16[512,2,128]{2,0,1:T(8,128)(2,1)S(1)}, bf16[512,2,128]{2,0,1:T(8,128)(2,1)}, u32[]{:S(2)}) copy-start(bf16[512,2,128]{2,0,1:T(8,128)(2,1)} %copy-done.1) | copy-start | bytes 786436
  114.3 3.2 copy-start.3
  122.3 3.2 copy-start.3
  130.3 3.2 copy-start.3
  138.3 3.2 copy-start.3
  145.1 6.1 %copy-start.6 = (bf16[512,2,128]{2,1,0:T(2,128)(2,1)S(1)}, bf16[512,2,128]{2,1,0:T(2,128)(2,1)}, u32[]{:S(2)}) copy-start(bf16[512,2,128]{2,1,0:T(2,128)(2,1)} %copy.36) | copy-start | bytes 786436
  151.2 126.4 %reduce-scatter.11.cloned.1.call-start = ((), (), s32[]{:S(2)}) async-start(), calls=%async_computation.13 | async-start | bytes 1310720 | tf_op jit(solution)/shard_map/reduce_scatter | solution.py:92
  217.2 3.7 copy-start.5
  220.7 87.1 %reduce-scatter.7.cloned.1.call-start = ((), (), s32[]{:S(2)}) async-start(), calls=%async_computation.11 | async-start | bytes 2359296 | tf_op jit(solution)/shard_map/reduce_scatter | solution.py:183
  267.1 103.4 %reduce-scatter.9.cloned.1.call-start = ((), (), s32[]{:S(2)}) async-start(), calls=%async_computation.12 | async-start | bytes 3932160 | tf_op jit(solution)/shard_map/reduce_scatter | solution.py:179
  273.2 1.0 copy-start.9
  273.3 142.0 %reduce-scatter.5.cloned.1.call-start = ((), (), s32[]{:S(2)}) async-start(), calls=%async_computation.7 | async-start | bytes 2359296 | tf_op jit(solution)/shard_map/reduce_scatter | solution.py:82
  277.6 30.2 %copy-start.8 = (bf16[64,2048]{1,0:T(8,128)(2,1)S(1)}, bf16[64,2048]{1,0:T(8,128)(2,1)}, u32[]{:S(2)}) copy-start(bf16[64,2048]{1,0:T(8,128)(2,1)} %param.13) | copy-start | bytes 786436
  (2 other events, 1.8 us)
Sparse Core Ops, SparseCore 0:
  11.2 30.4 all-gather.6
  48.9 27.9 all-gather.8
  78.5 27.3 all-gather.10
  107.6 27.1 all-gather.12
  136.8 28.0 all-gather.14
  166.3 27.3 all-gather.16
  220.8 26.5 reduce-scatter.10
  267.2 40.4 reduce-scatter.6
  310.0 60.3 reduce-scatter.8
  374.2 41.0 reduce-scatter.4
where the time goes:
time: 424 us; the launch traced here: 422 us
  waiting for transfers between devices  202 us (48%)
  matrix products  109 us (26%)
  local copies, waits for them, and re-layouts  50.9 us (12%)
  blocking collectives  26.4 us (6%)
  other arithmetic  17.9 us (4%)
  between operations  15.3 us (4%)
    reduce_scatter x1, waiting for transfers between devices, per_device(): lax.psum_scatter(qkv_part.astype(jnp.bfloat16), 'row', scatter_dimension=...  59.7 us
    reduce_scatter x1, waiting for transfers between devices, per_device(): lax.psum_scatter(jnp.dot(rows, out_weight, preferred_element_type=jnp.flo...  42.2 us
    all_gather x1, waiting for transfers between devices, per_device(): group = lax.all_gather(hidden, 'col', axis=0, tiled=True)  30.6 us
    reduce_scatter x1, waiting for transfers between devices, per_device(): lax.psum_scatter(jnp.einsum('ksh,kdh->sd', rows, qkv_weight, preferred_el...  28.2 us
    all_gather x1, waiting for transfers between devices, per_device(): value_piece = lax.all_gather(value_heads, 'row', axis=0, tiled=True)  23.6 us
    dot_general x8, matrix products, pair_terms(): jnp.einsum('qhd,khd->hqk', query_rows, key_block, preferred_element_type=...  22.8 us
    all_gather x1, waiting for transfers between devices, per_device(): key_piece = lax.all_gather(key_heads, 'row', axis=0, tiled=True)  16.5 us
    unnamed x30, local copies, waits for them, and re-layouts  15.4 us
  transfers between devices with their start and end apart: 10, of which 6 were waited for; matrix products, arithmetic and copies ran while one was open for 39% of the time, Pallas kernels for 0%

commit v1 on v0

--- a/solution.py
+++ b/solution.py
@@ -52,8 +52,12 @@
         jnp.zeros((span, heads_here, head_dim), jnp.float32),
     )
     carry = start_state
-    key_piece = lax.all_gather(key_heads, "row", axis=0, tiled=True)
-    value_piece = lax.all_gather(value_heads, "row", axis=0, tiled=True)
+    name_matrix = lambda incoming_x, block_here, mesh_ax: jnp.split(
+        lax.all_gather(jnp.concatenate([incoming_x, block_here], 1), mesh_ax, axis=0, tiled=True),
+        [incoming_x.shape[1]],
+        1,
+    )
+    key_piece, value_piece = name_matrix(key_heads, value_heads, "row")
     size = math.gcd(key_piece.shape[0], 512)
 
     def attend_step(state, block):

time: 424 us -> 466 us (1.099)
  waiting for transfers between devices: 202 us -> 247 us
    all_gather x0 -> x1, waiting for transfers between devices: none -> 43.4 us  [per_device(): lax.all_gather(jnp.concatenate([incoming_x, block_here], 1), mesh_ax, axi...]
    dynamic_slice x8 -> x0, local copies, waits for them, and re-layouts: 8 us -> none  [per_device(): lax.scan(attend_step, carry, (split_blocks(key_piece, size), split_blocks...]
    unnamed x30 -> x33, local copies, waits for them, and re-layouts: 15.4 us -> 17 us
  transfers between devices with their start and end apart: 10 -> 11, of which waited for: 6 -> 7; matrix products, arithmetic and copies ran while one was open for 39% -> 35% of each run, Pallas kernels for 0% -> 0%
where the time goes in v1:
time: 466 us; the launch traced here: 464 us
  waiting for transfers between devices  247 us (53%)
  matrix products  109 us (23%)
  local copies, waits for them, and re-layouts  46.4 us (10%)
  blocking collectives  26.6 us (6%)
  other arithmetic  19.8 us (4%)
  between operations  15 us (3%)
    reduce_scatter x1, waiting for transfers between devices, per_device(): lax.psum_scatter(qkv_part.astype(jnp.bfloat16), 'row', scatter_dimension=...  59.5 us
    all_gather x1, waiting for transfers between devices, per_device(): lax.all_gather(jnp.concatenate([incoming_x, block_here], 1), mesh_ax, axi...  43.4 us
    reduce_scatter x1, waiting for transfers between devices, per_device(): lax.psum_scatter(jnp.dot(rows, out_weight, preferred_element_type=jnp.flo...  42.4 us
    all_gather x1, waiting for transfers between devices, per_device(): group = lax.all_gather(hidden, 'col', axis=0, tiled=True)  30.6 us
    reduce_scatter x1, waiting for transfers between devices, per_device(): lax.psum_scatter(jnp.einsum('ksh,kdh->sd', rows, qkv_weight, preferred_el...  27.5 us
    all_gather x1, waiting for transfers between devices, per_device(): value_piece = lax.all_gather(value_heads, 'row', axis=0, tiled=True)  27.2 us
    dot_general x8, matrix products, pair_terms(): jnp.einsum('qhd,khd->hqk', query_rows, key_block, preferred_element_type=...  22.7 us
    unnamed x33, local copies, waits for them, and re-layouts  17 us
  transfers between devices with their start and end apart: 11, of which 7 were waited for; matrix products, arithmetic and copies ran while one was open for 35% of the time, Pallas kernels for 0%

profile of v1, /device:TPU:0, one launch (start us, length us, event | category | flops | bytes accessed | tf_op | source)
XLA Modules:
  0.0 464.2 jit_solution(14620670859042457299)
XLA Ops:
  11.1 30.6 %all-gather.8.cloned.1.call-done = bf16[512,2048]{1,0:T(8,128)(2,1)} async-done(((bf16[64,2048]{1,0:T(8,128)(2,1)}), bf16[512,2048]{1,0:T(8,128)(2,1)}) %all-gather.8.cloned.1.call-update) | async-done | bytes 2097168 | tf_op jit(solution)/shard_map/all_gather | solution.py:43
  41.7 3.4 fusion.56
  60.4 15.4 %all-gather.12.cloned.1.call-done = bf16[2048,2,128]{0,2,1:T(8,128)(2,1)} async-done(((bf16[512,2,128]{0,2,1:T(8,128)(2,1)}), bf16[2048,2,128]{0,2,1:T(8,128)(2,1)}) %all-gather.12.cloned.1.call-update) | async-done | bytes 1048592 | tf_op jit(solution)/shard_map/all_gather | solution.py:122
  78.2 27.2 %all-gather.14.cloned.1.call-done = bf16[2048,2,128]{0,2,1:T(8,128)(2,1)} async-done(((bf16[512,2,128]{0,2,1:T(8,128)(2,1)}), bf16[2048,2,128]{0,2,1:T(8,128)(2,1)}) %all-gather.14.cloned.1.call-update) | async-done | bytes 1048592 | tf_op jit(solution)/shard_map/all_gather | solution.py:123
  105.4 3.7 copy.58
  109.1 43.4 %all-gather.10.cloned.1.call-done = bf16[2048,4,128]{0,2,1:T(8,128)(2,1)} async-done(((bf16[512,4,128]{0,2,1:T(8,128)(2,1)}), bf16[2048,4,128]{0,2,1:T(8,128)(2,1)}) %all-gather.10.cloned.1.call-update) | async-done | bytes 2097168 | tf_op jit(solution)/shard_map/all_gather | solution.py:56
  163.4 23.6 %while.37 = (s32[]{:T(128)}, f32[2,512]{1,0:T(2,128)S(1)}, f32[512,2,128]{0,2,1:T(8,128)}, bf16[4,512,2,128]{3,1,2,0:T(8,128)(2,1)}, bf16[512,2,128]{2,0,1:T(8,1...) while((s32[]{:T(128)}, f32[2,512]{1,0:T(2,128)S(1)}, ...), condition=%wide.region_6.7_spmd.clone, body=%wide.region_4.6_spmd.clone.sunk | while | flops 271844352 | bytes 6046864 | solution.py:79
  187.0 3.6 multiply_reduce_fusion.3
  194.3 33.0 %while.38 = (s32[]{:T(128)}, f32[512,2,128]{0,2,1:T(8,128)}, bf16[4,512,2,128]{1,3,2,0:T(8,128)(2,1)}, bf16[512,2,128]{2,1,0:T(2,128)(2,1)S(1)}, f32[2]{0:T(128)...) while((s32[]{:T(128)}, f32[512,2,128]{0,2,1:T(8,128)}, ...), condition=%wide.region_10.11_spmd.clone, body=%wide.region_9.10_spmd.clone.sunk | while | flops 406585344 | bytes 7087251 | solution.py:135
  199.0 3.6 fusion.113
  207.2 3.6 fusion.113
  215.5 3.6 fusion.113
  223.7 3.7 fusion.113
  233.7 13.4 %all_gather.35 = f32[2048,2]{0,1:T(2,128)S(1)} all-gather(f32[512,2]{0,1:T(2,128)S(1)} %get-tuple-element.731), channel_id=1, replica_groups=mesh['row'=4,'col'=8] {'row'}, dimensions={0}, use_global_device_ids=true | all-gather | bytes 20480 | tf_op jit(solution)/shard_map/all_gather | solution.py:141
  247.1 13.2 %all_gather.33 = f32[2048,2]{0,1:T(2,128)S(1)} all-gather(f32[512,2]{0,1:T(2,128)S(1)} %fusion.84), channel_id=1, replica_groups=mesh['row'=4,'col'=8] {'row'}, dimensions={0}, use_global_device_ids=true | all-gather | bytes 20480 | tf_op jit(solution)/shard_map/all_gather | solution.py:140
  260.3 3.4 convolution_convert_fusion.2
  264.0 36.5 %while.39 = (s32[]{:T(128)}, f32[512,2,128]{0,2,1:T(8,128)}, f32[512,2,128]{0,2,1:T(8,128)}, bf16[4,512,2,128]{3,1,0,2:T(8,128)(2,1)}, bf16[512,2,128]{2,0,1:T(8...) while((s32[]{:T(128)}, f32[512,2,128]{0,2,1:T(8,128)}, ...), condition=%wide.region_13.14_spmd.clone, body=%wide.region_12.13_spmd.clone.sunk | while | flops 541589504 | bytes 9988260 | solution.py:165
  279.0 3.3 fusion.121
  305.9 4.3 bitcast_convert_fusion.2
  311.2 5.3 %fusion.52 = bf16[3,2048,256]{1,2,0:T(8,128)(2,1)} fusion(bf16[512,2048]{1,0:T(8,128)(2,1)} %all-gather.8.cloned.1.call-done, bf16[1,512,256]{2,1,0:T(8,128)(2,1)} %copy.60, bf16[1,512,256]{2,1,0:T(8,128)(2,1)} %copy.59, bf16[1,512,256]{2,1,0:T(8,128)(2,1)S(1)} %copy-done.11), kind=kOutput, calls=%fused_computation.61 | convolution fusion | flops 1612972032 | bytes 6029312 | tf_op jit(solution)/shard_map/sd,ksh->kdh/dot_general | solution.py:182
  317.4 3.4 convolution_convert_fusion.1
  322.7 27.5 %reduce-scatter.7.cloned.1.call-done = bf16[64,2048]{1,0:T(8,128)(2,1)} async-done(((bf16[512,2048]{1,0:T(8,128)(2,1)}), bf16[64,2048]{1,0:T(8,128)(2,1)}) %reduce-scatter.7.cloned.1.call-update) | async-done | bytes 262160 | tf_op jit(solution)/shard_map/reduce_scatter | solution.py:187
  353.2 59.5 %reduce-scatter.9.cloned.1.call-done = bf16[3,512,256]{1,2,0:T(8,128)(2,1)} async-done(((bf16[3,2048,256]{1,2,0:T(8,128)(2,1)}), bf16[3,512,256]{1,2,0:T(8,128)(2,1)}) %reduce-scatter.9.cloned.1.call-update) | async-done | bytes 786448 | tf_op jit(solution)/shard_map/reduce_scatter | solution.py:183
  415.3 42.4 %reduce-scatter.5.cloned.1.call-done = bf16[64,2048]{1,0:T(8,128)(2,1)} async-done(((bf16[512,2048]{1,0:T(8,128)(2,1)}), bf16[64,2048]{1,0:T(8,128)(2,1)}) %reduce-scatter.5.cloned.1.call-update) | async-done | bytes 262160 | tf_op jit(solution)/shard_map/reduce_scatter | solution.py:86
  (139 shorter events, 131.7 us)
Async XLA Ops:
  7.2 34.6 %copy-start = (bf16[3,2048,256]{2,1,0:T(8,128)(2,1)S(1)}, bf16[3,2048,256]{2,1,0:T(8,128)(2,1)}, u32[]{:S(2)}) copy-start(bf16[3,2048,256]{2,1,0:T(8,128)(2,1)} %param.16) | copy-start | bytes 9437188
  7.2 2.9 copy-start.6
  7.2 34.5 %all-gather.8.cloned.1.call-start = ((), (), s32[]{:S(2)}) async-start(), calls=%async_computation.4 | async-start | bytes 2359296 | tf_op jit(solution)/shard_map/all_gather | solution.py:43
  11.1 64.8 %all-gather.12.cloned.1.call-start = ((), (), s32[]{:S(2)}) async-start(), calls=%async_computation.7 | async-start | bytes 1310720 | tf_op jit(solution)/shard_map/all_gather | solution.py:122
  45.2 1.3 copy-start.10
  46.1 0.8 copy-start.3
  46.1 6.1 %copy-start.12 = (f32[2]{0:T(128)S(1)}, f32[2]{0:T(128)}, u32[]{:S(2)}) copy-start(f32[2]{0:T(128)} %param.17) | copy-start | bytes 28
  47.7 4.5 copy-start.8
  47.7 57.7 %all-gather.14.cloned.1.call-start = ((), (), s32[]{:S(2)}) async-start(), calls=%async_computation.8 | async-start | bytes 1310720 | tf_op jit(solution)/shard_map/all_gather | solution.py:123
  49.6 102.9 %all-gather.10.cloned.1.call-start = ((), (), s32[]{:S(2)}) async-start(), calls=%async_computation.5 | async-start | bytes 2621440 | tf_op jit(solution)/shard_map/all_gather | solution.py:56
  51.5 135.5 %all-gather.16.cloned.1.call-start = ((), (), s32[]{:S(2)}) async-start(), calls=%async_computation.9 | async-start | bytes 2359296 | tf_op jit(solution)/shard_map/all_gather | solution.py:92
  52.1 211.8 %all-gather.18.cloned.1.call-start = ((), (), s32[]{:S(2)}) async-start(), calls=%async_computation.10 | async-start | bytes 1310720 | tf_op jit(solution)/shard_map/all_gather | solution.py:144
  59.3 1.0 copy-start.1
  60.4 203.6 %all-gather.20.cloned.1.call-start = ((), (), s32[]{:S(2)}) async-start(), calls=%async_computation.11 | async-start | bytes 1310720 | tf_op jit(solution)/shard_map/all_gather | solution.py:145
  158.3 5.1 %copy-start.2 = (bf16[512,2,128]{2,0,1:T(8,128)(2,1)S(1)}, bf16[512,2,128]{2,0,1:T(8,128)(2,1)}, u32[]{:S(2)}) copy-start(bf16[512,2,128]{2,0,1:T(8,128)(2,1)} %copy-done.1) | copy-start | bytes 786436
  187.0 7.3 %copy-start.5 = (bf16[512,2,128]{2,1,0:T(2,128)(2,1)S(1)}, bf16[512,2,128]{2,1,0:T(2,128)(2,1)}, u32[]{:S(2)}) copy-start(bf16[512,2,128]{2,1,0:T(2,128)(2,1)} %copy.35) | copy-start | bytes 786436
  194.3 126.5 %reduce-scatter.11.cloned.1.call-start = ((), (), s32[]{:S(2)}) async-start(), calls=%async_computation.14 | async-start | bytes 1310720 | tf_op jit(solution)/shard_map/reduce_scatter | solution.py:96
  260.3 3.7 copy-start.4
  263.7 86.5 %reduce-scatter.7.cloned.1.call-start = ((), (), s32[]{:S(2)}) async-start(), calls=%async_computation.12 | async-start | bytes 2359296 | tf_op jit(solution)/shard_map/reduce_scatter | solution.py:187
  310.2 0.9 copy-start.11
  310.2 102.5 %reduce-scatter.9.cloned.1.call-start = ((), (), s32[]{:S(2)}) async-start(), calls=%async_computation.13 | async-start | bytes 3932160 | tf_op jit(solution)/shard_map/reduce_scatter | solution.py:183
  316.4 1.0 copy-start.9
  316.5 141.2 %reduce-scatter.5.cloned.1.call-start = ((), (), s32[]{:S(2)}) async-start(), calls=%async_computation.6 | async-start | bytes 2359296 | tf_op jit(solution)/shard_map/reduce_scatter | solution.py:86
  320.8 29.4 %copy-start.7 = (bf16[64,2048]{1,0:T(8,128)(2,1)S(1)}, bf16[64,2048]{1,0:T(8,128)(2,1)}, u32[]{:S(2)}) copy-start(bf16[64,2048]{1,0:T(8,128)(2,1)} %param.13) | copy-start | bytes 786436
Sparse Core Ops, SparseCore 0:
  11.2 30.4 all-gather.7
  47.8 27.9 all-gather.11
  78.0 27.3 all-gather.13
  107.4 45.0 all-gather.9
  154.2 26.5 all-gather.15
  182.2 27.9 all-gather.17
  211.8 27.4 all-gather.19
  263.8 25.8 reduce-scatter.10
  310.4 39.7 reduce-scatter.6
  352.3 60.3 reduce-scatter.8
  416.6 40.9 reduce-scatter.4
